TPU v7x, 32 devices: a whole 2x2x4 slice. The times are simulated.
32 devices in a mesh: batch: 4 (over y, x), heads: 8 (over z, core).
Axes of the slice: x: 2, y: 2, z: 4, core: 2. Of those that a mesh axis runs over, the one named last changes fastest.
Arguments:
- draft_ids: int32 [192, 8], P('batch'), may hold values from 0 to 50279
- accepted: int32 [192], P('batch'), may hold values from 1 to 8
- embedding: bfloat16 [50280, 2560], P(None, 'heads'), may hold values from -6 to 6
- norm_gain: float32 [2, 2560], replicated, may hold values from 0.5 to 1.5
- w_zx: bfloat16 [2, 2560, 8, 128], P(None, None, 'heads'), may hold values from -0.125 to 0.125
- w_dt: bfloat16 [2, 2560, 8], P(None, None, 'heads'), may hold values from -0.125 to 0.125
- w_bc: bfloat16 [2, 2560, 256], P(None, None, 'heads'), may hold values from -0.125 to 0.125
- dt_bias: float32 [2, 8], P(None, 'heads'), may hold values from -4 to -1
- decay_rate: float32 [2, 8], P(None, 'heads'), may hold values from 1 to 16
- skip_weight: float32 [2, 8], P(None, 'heads'), may hold values from 0.5 to 1.5
- conv_x_w: bfloat16 [2, 4, 512], P(None, None, 'heads'), may hold values from -3 to 3
- conv_x_b: bfloat16 [2, 512], P(None, 'heads'), may hold values from -3 to 3
- conv_bc_w: bfloat16 [2, 4, 256], P(None, None, 'heads'), may hold values from -3 to 3
- conv_bc_b: bfloat16 [2, 256], P(None, 'heads'), may hold values from -3 to 3
- gate_gain: float32 [2, 512], P(None, 'heads'), may hold values from 0.5 to 1.5
- out_w: bfloat16 [2, 512, 2560], P(None, 'heads'), may hold values from -0.375 to 0.375
- ssm_state: float32 [2, 192, 8, 64, 128], P(None, 'batch', 'heads'), may hold values from -1.6 to 1.6
- conv_x_state: bfloat16 [2, 192, 3, 512], P(None, 'batch', None, 'heads'), may hold values from -6 to 6
- conv_bc_state: bfloat16 [2, 192, 3, 256], P(None, 'batch', None, 'heads'), may hold values from -6 to 6
Outputs:
- hidden_out: bfloat16 [1536, 2560], P('batch', 'heads')
- new_ssm: float32 [2, 192, 8, 64, 128], P(None, 'batch', 'heads')
- new_conv_x: bfloat16 [2, 192, 3, 512], P(None, 'batch', None, 'heads')
- new_conv_bc: bfloat16 [2, 192, 3, 256], P(None, 'batch', None, 'heads')
Inputs may be any that keep to these rules, and one draw needn't show every extreme that they name: `accepted`: the number of a sequence's draft tokens that are kept, counted from the first.
All inputs are finite; a program needn't handle non-finite values.
Results may differ from a plain program's by a relative error of at most 0.015.
Values may be sent and summed in bfloat16 or wider, within the bound.
A program may use at most 128 MiB of HBM per device.

v0:
```python
import jax
import jax.numpy as jnp
from jax import lax
from jax.sharding import PartitionSpec as P

LAYERS = 2
EPS = 1e-05


def rms_scale(total, count):
    return lax.rsqrt(total / count + EPS)


def convolve(window, weight, bias, count):
    weight = weight.astype(jnp.float32)
    acc = window[:, 0:count] * weight[0]
    for k in range(1, weight.shape[0]):
        acc = acc + window[:, k : k + count] * weight[k]
    return jax.nn.silu(acc + bias.astype(jnp.float32))


def keep_rows(window, accepted, kept_rows):
    last_start = window.shape[1] - kept_rows
    kept = window[:, 1 : 1 + kept_rows]
    for start in range(2, last_start + 1):
        kept = jnp.where(
            (accepted == start)[:, None, None], window[:, start : start + kept_rows], kept
        )
    return kept


def recur(decay, step, values, bmat, cmat, skip, state, accepted):
    kept = state
    outputs = []
    for t in range(values.shape[1]):
        state = (
            decay[:, t, None, None] * state
            + (step[:, t, None] * values[:, t])[:, :, None] * bmat[:, t, None, :]
        )
        outputs.append(jnp.sum(state * cmat[:, t, None, :], axis=-1) + skip * values[:, t])
        kept = jnp.where((accepted == t + 1)[:, None, None], state, kept)
    return (jnp.stack(outputs, 1), kept)


def spread_terms(u_rows, scale, weight):
    product = lax.dot_general(
        weight, u_rows, (((0,), (1,)), ((), ())), preferred_element_type=jnp.float32
    )
    return product * scale[None, :]


def token_scale(local_sq, inner):
    return rms_scale(lax.psum(local_sq, "heads"), inner)


def local(
    draft_ids,
    accepted,
    embedding,
    norm_gain,
    w_zx,
    w_dt,
    w_bc,
    dt_bias,
    decay_rate,
    skip_weight,
    conv_x_w,
    conv_x_b,
    conv_bc_w,
    conv_bc_b,
    gate_gain,
    out_w,
    ssm_state,
    conv_x_state,
    conv_bc_state,
):
    seq_rows, draft = draft_ids.shape
    heads_here = w_zx.shape[2]
    width = w_zx.shape[3] // 2
    local_inner = heads_here * width
    own_cols = embedding.shape[1]
    model = own_cols * lax.axis_size("heads")
    inner = local_inner * lax.axis_size("heads")
    bc_here = w_bc.shape[2]
    kernel = conv_x_w.shape[1]
    recur_heads = jax.vmap(recur, in_axes=(2, 2, 2, None, None, 0, 1, None), out_axes=(2, 1))
    whole_bc = (
        lax.all_gather(w_bc, "heads", axis=2, tiled=True),
        lax.all_gather(conv_bc_w, "heads", axis=2, tiled=True),
        lax.all_gather(conv_bc_b, "heads", axis=1, tiled=True),
        lax.all_gather(conv_bc_state, "heads", axis=3, tiled=True),
    )
    saved_state, saved_x, saved_bc = ([], [], [])

    def mixer(layer, stream):
        value = stream.astype(jnp.float32)
        normed = (
            value * rms_scale(jnp.sum(value * value, -1, keepdims=True), model) * norm_gain[layer]
        ).astype(jnp.bfloat16)
        zx = jnp.dot(
            normed, w_zx[layer].reshape(model, -1), preferred_element_type=jnp.float32
        ).astype(jnp.bfloat16)
        zx = zx.reshape(seq_rows, draft, heads_here, 2, width)
        gate_z = zx[:, :, :, 0].astype(jnp.float32)
        values = zx[:, :, :, 1].reshape(seq_rows, draft, local_inner)
        dt_raw = (
            jnp.dot(normed, w_dt[layer], preferred_element_type=jnp.float32)
            .astype(jnp.bfloat16)
            .reshape(seq_rows, draft, heads_here)
        )
        bc = (
            jnp.dot(normed, whole_bc[0][layer], preferred_element_type=jnp.float32)
            .astype(jnp.bfloat16)
            .reshape(seq_rows, draft, -1)
        )
        window_bc = jnp.concatenate([whole_bc[3][layer], bc], axis=1)
        bcc = convolve(
            window_bc.astype(jnp.float32), whole_bc[1][layer], whole_bc[2][layer], draft
        ).astype(jnp.bfloat16)
        kept_bc = keep_rows(window_bc, accepted, kernel - 1)
        bcc = lax.optimization_barrier(bcc).astype(jnp.float32)
        kept_bc = lax.dynamic_slice_in_dim(kept_bc, lax.axis_index("heads") * bc_here, bc_here, 2)
        states = bcc.shape[2] // 2
        bmat = bcc[..., :states]
        cmat = bcc[..., states:]
        window_x = jnp.concatenate([conv_x_state[layer], values], axis=1)
        xc = convolve(
            window_x.astype(jnp.float32), conv_x_w[layer], conv_x_b[layer], draft
        ).reshape(seq_rows, draft, heads_here, width)
        step = jax.nn.softplus(dt_raw.astype(jnp.float32) + dt_bias[layer])
        decay = jnp.exp(-step * decay_rate[layer])
        outputs, kept = recur_heads(
            decay, step, xc, bmat, cmat, skip_weight[layer], ssm_state[layer], accepted
        )
        saved_state.append(kept)
        saved_x.append(keep_rows(window_x, accepted, kernel - 1))
        saved_bc.append(kept_bc)
        gated = outputs * jax.nn.silu(gate_z)
        local_sq = jnp.sum(gated * gated, axis=(2, 3)).reshape(-1)
        u_rows = (
            (gated.reshape(seq_rows, draft, local_inner) * gate_gain[layer])
            .astype(jnp.bfloat16)
            .reshape(-1, local_inner)
        )
        return (u_rows, local_sq)

    part = embedding[draft_ids.reshape(-1)]
    stream = lax.all_gather(part, "heads", axis=1, tiled=True)
    where_cols = lax.axis_index("heads") * own_cols
    result = part
    for layer in range(LAYERS):
        u_rows, local_sq = mixer(layer, stream)
        scale = token_scale(local_sq, inner)
        if layer + 1 < LAYERS:
            term = (
                jnp.dot(u_rows, out_w[layer], preferred_element_type=jnp.float32) * scale[:, None]
            )
            total = lax.psum(term, "heads")
            stream = (stream.astype(jnp.float32) + total).astype(jnp.bfloat16)
        else:
            mine = lax.psum_scatter(
                spread_terms(u_rows, scale, out_w[layer]), "heads", scatter_dimension=0, tiled=True
            )
            own_stream = lax.dynamic_slice_in_dim(stream, where_cols, own_cols, 1)
            result = (own_stream.astype(jnp.float32) + mine.T).astype(jnp.bfloat16)
    return (result, jnp.stack(saved_state), jnp.stack(saved_x), jnp.stack(saved_bc))


def solution(mesh):
    placed = (
        P("batch", None),
        P("batch"),
        P(None, "heads"),
        P(),
        P(None, None, "heads", None),
        P(None, None, "heads"),
        P(None, None, "heads"),
        P(None, "heads"),
        P(None, "heads"),
        P(None, "heads"),
        P(None, None, "heads"),
        P(None, "heads"),
        P(None, None, "heads"),
        P(None, "heads"),
        P(None, "heads"),
        P(None, "heads", None),
        P(None, "batch", "heads", None, None),
        P(None, "batch", None, "heads"),
        P(None, "batch", None, "heads"),
    )
    return jax.shard_map(
        local,
        mesh=mesh,
        in_specs=placed,
        out_specs=(
            P("batch", "heads"),
            P(None, "batch", "heads", None, None),
            P(None, "batch", None, "heads"),
            P(None, "batch", None, "heads"),
        ),
        check_vma=False,
    )
```

profile of v0, /device:TPU:0, one launch (start us, length us, event | category | flops | bytes accessed | tf_op | source)
XLA Modules:
  0.0 371.8 jit_solution(4346947506731001234)
XLA Ops:
  7.2 43.7 %copy.113 = bf16[50280,320]{1,0:T(8,128)(2,1)} copy(bf16[50280,320]{0,1:T(8,128)(2,1)} %param.21) | data formatting | bytes 64358400 | tf_op args[2]
  51.2 7.8 %gather_fusion = bf16[384,320]{1,0:T(8,128)(2,1)S(1)} fusion(bf16[50280,320]{1,0:T(8,128)(2,1)} %copy.113, s32[1024]{0:T(1024)S(1)} %pad_clamp_fusion), kind=kCustom, calls=%fused_computation | custom fusion | bytes 493056 | tf_op jit(solution)/shard_map/gather | solution.py:147
  60.8 16.7 %all_gather.16 = bf16[2,48,3,256]{1,3,2,0:T(8,128)(2,1)S(1)} all-gather(bf16[2,48,3,32]{1,3,2,0:T(8,128)(2,1)S(1)} %copy-done.48), channel_id=1, replica_groups=mesh['batch'=4,'heads'=8] {'heads'}, dimensions={3}, use_global_device_ids=true | all-gather | bytes 165888 | tf_op jit(solution)/shard_map/all_gather | solution.py:91
  77.9 15.1 %all_gather.18 = bf16[2,4,256]{1,0,2:T(2,128)(2,1)S(1)} all-gather(bf16[2,4,32]{1,0,2:T(2,128)(2,1)S(1)} %copy.118), channel_id=1, replica_groups=mesh['batch'=4,'heads'=8] {'heads'}, dimensions={2}, use_global_device_ids=true | all-gather | bytes 4608 | tf_op jit(solution)/shard_map/all_gather | solution.py:89
  93.0 12.0 %all-gather.1 = bf16[8,32,2]{1,2,0:T(2,128)(2,1)S(1)} all-gather(bf16[1,32,2]{1,2,0:T(2,128)(2,1)S(1)} %bitcast.580), channel_id=1, replica_groups=mesh['batch'=4,'heads'=8] {'heads'}, dimensions={0}, use_global_device_ids=true | all-gather | bytes 1152 | tf_op jit(solution)/shard_map/all_gather | solution.py:90
  107.1 2.9 slice_reduce_fusion.7
  111.3 2.7 copy.115
  119.7 7.5 %all-gather.5.cloned.1.call-done = bf16[2,2560,256]{1,2,0:T(8,128)(2,1)} async-done(((bf16[2,2560,32]{1,2,0:T(8,128)(2,1)}), bf16[2,2560,256]{1,2,0:T(8,128)(2,1)}) %all-gather.5.cloned.1.call-update) | async-done | bytes 2621456 | tf_op jit(solution)/shard_map/all_gather | solution.py:88
  131.2 4.1 %multiply_add_fusion.8 = (f32[1,48,64,128]{3,2,1,0:T(8,128)S(1)}, f32[1,48,64,128]{3,2,1,0:T(8,128)S(1)}, f32[48,64]{1,0:T(8,128)S(1)}, f32[48,64]{1,0:T(8,128)S(1)}) fusion(f32[48,128]{1,0:T(8,128)S(1)} %bitcast.537, f32[48,64]{1,0:T(8,128)S(1)} %get-tuple-element.186, f32[48]{0:T(128)S(1)} %get-tuple-element.237, f32[48,128]{1,0:T(8,128)S(1)} %bitcast.525, ...), kind=kLoop, calls=%fused_computation.43 | loop fusion | flops 7464960 | bytes 4977600 | tf_op jit(solution)/shard_map/vmap()/add | solution.py:37
  139.5 3.7 multiply_reduce_fusion.8
  145.9 15.0 %psum.21 = f32[384]{0:T(512)S(1)} all-reduce(f32[384]{0:T(512)S(1)} %reshape.2511), channel_id=1, replica_groups=mesh['batch'=4,'heads'=8] {'heads'}, use_global_device_ids=true, to_apply=%region_10.11 | all-reduce | flops 384 | bytes 3072 | tf_op jit(solution)/shard_map/psum | solution.py:53
  160.9 3.5 convolution_multiply_fusion.1
  165.6 2.9 slice_reduce_fusion.3
  168.5 85.9 %all-reduce.2.cloned.1.call-done = f32[384,2560]{1,0:T(8,128)} async-done(((f32[384,2560]{1,0:T(8,128)}), f32[384,2560]{1,0:T(8,128)}) %all-reduce.2.cloned.1.call-update) | async-done | bytes 3932176 | tf_op jit(solution)/shard_map/psum | solution.py:158
  254.3 2.9 fusion.1
  264.7 2.1 fusion.14
  268.8 4.1 %multiply_add_fusion.2 = (f32[1,48,64,128]{3,2,1,0:T(8,128)S(1)}, f32[1,48,64,128]{3,2,1,0:T(8,128)S(1)}, f32[48,64]{1,0:T(8,128)S(1)}, f32[48,64]{1,0:T(8,128)S(1)}) fusion(f32[48,128]{1,0:T(8,128)S(1)} %bitcast.551, f32[48,64]{1,0:T(8,128)S(1)} %get-tuple-element.160, f32[48]{0:T(128)S(1)} %get-tuple-element.51, f32[48,128]{1,0:T(8,128)S(1)} %bitcast.528, ...), kind=kLoop, calls=%fused_computation.29 | loop fusion | flops 7464960 | bytes 4977600 | tf_op jit(solution)/shard_map/vmap()/add | solution.py:37
  279.5 3.7 multiply_reduce_fusion
  290.3 15.7 %psum.23 = f32[384]{0:T(512)S(1)} all-reduce(f32[384]{0:T(512)S(1)} %reshape.2516), channel_id=1, replica_groups=mesh['batch'=4,'heads'=8] {'heads'}, use_global_device_ids=true, to_apply=%region_22.23 | all-reduce | flops 384 | bytes 3072 | tf_op jit(solution)/shard_map/psum | solution.py:53
  307.1 3.5 fusion
  310.6 5.6 %copy.139 = f32[2560,384]{1,0:T(8,128)} copy(f32[2560,384]{0,1:T(8,128)} %fusion) | data formatting | bytes 7864320
  322.0 9.0 %select_select_fusion.1 = f32[1,48,1,64,128]{4,3,2,1,0:T(8,128)} fusion(f32[2,48,1,64,128]{4,3,2,1,0:T(8,128)S(1)} %copy-done.1, f32[48,128]{1,0:T(8,128)} %bitcast.536, f32[48,64]{1,0:T(8,128)} %copy-done.34, f32[48,128]{1,0:T(8,128)} %bitcast.534, f32[48,64]{1,0:T(8,128)} %copy-done.35, f32[48,128]{1,0:T(8,128)} %bitcast.532, f32[48,64]{1,0:T(8,128)} %copy-done.33, ...), kind=kLoop, calls=%fused_computation.22 | loop fusion | flops 12582912 | bytes 3442560 | tf_op jit(solution)/shard_map/vmap(jit(_where))/select_n | solution.py:41
  336.1 8.2 %select_select_fusion = f32[1,48,1,64,128]{4,3,2,1,0:T(8,128)S(1)} fusion(f32[2,48,1,64,128]{4,3,2,1,0:T(8,128)S(1)} %copy-done.1, f32[48,128]{1,0:T(8,128)} %bitcast.550, f32[48,64]{1,0:T(8,128)} %copy-done.40, f32[48,128]{1,0:T(8,128)} %bitcast.548, f32[48,64]{1,0:T(8,128)} %copy-done.42, f32[48,128]{1,0:T(8,128)} %bitcast.546, f32[48,64]{1,0:T(8,128)} %copy-done.41, ...), kind=kLoop, calls=%fused_computation.21 | loop fusion | flops 12582912 | bytes 3442560 | tf_op jit(solution)/shard_map/vmap(jit(_where))/select_n | solution.py:41
  346.3 15.7 %reduce-scatter.4.cloned.1.call-done = f32[320,384]{1,0:T(8,128)} async-done(((f32[2560,384]{1,0:T(8,128)}), f32[320,384]{1,0:T(8,128)}) %reduce-scatter.4.cloned.1.call-update) | async-done | bytes 491536
  (283 shorter events, 62.2 us)
Async XLA Ops:
  7.2 43.8 %copy-start.73 = (s32[48,8]{0,1:T(8,128)S(1)}, s32[48,8]{0,1:T(8,128)}, u32[]{:S(2)}) copy-start(s32[48,8]{0,1:T(8,128)} %param.19) | copy-start | bytes 4612
  7.2 104.1 %all-gather.7.cloned.1.call-start = ((), (), s32[]{:S(2)}) async-start(), calls=%async_computation.3 | async-start | bytes 2211840 | tf_op jit(solution)/shard_map/all_gather | solution.py:148
  59.0 18.7 %copy-start.75 = (bf16[2,4,32]{2,1,0:T(4,128)(2,1)S(1)}, bf16[2,4,32]{2,1,0:T(4,128)(2,1)}, u32[]{:S(2)}) copy-start(bf16[2,4,32]{2,1,0:T(4,128)(2,1)} %param.31) | copy-start | bytes 1540
  59.0 34.0 %copy-start.82 = (bf16[2,32]{1,0:T(2,128)(2,1)S(1)}, bf16[2,32]{1,0:T(2,128)(2,1)}, u32[]{:S(2)}) copy-start(bf16[2,32]{1,0:T(2,128)(2,1)} %param.32) | copy-start | bytes 388
  59.0 46.1 %copy-start.77 = (f32[2,1]{0,1:T(1,128)S(1)}, f32[2,1]{0,1:T(1,128)}, u32[]{:S(2)}) copy-start(f32[2,1]{0,1:T(1,128)} %param.26) | copy-start | bytes 28
  59.0 46.7 %copy-start.78 = (f32[2,1]{0,1:T(1,128)S(1)}, f32[2,1]{0,1:T(1,128)}, u32[]{:S(2)}) copy-start(f32[2,1]{0,1:T(1,128)} %param.27) | copy-start | bytes 28
  59.1 47.3 %copy-start.79 = (f32[2,1]{0,1:T(1,128)S(1)}, f32[2,1]{0,1:T(1,128)}, u32[]{:S(2)}) copy-start(f32[2,1]{0,1:T(1,128)} %param.28) | copy-start | bytes 28
  59.1 47.8 %copy-start.55 = (f32[2,2560]{1,0:T(2,128)S(1)}, f32[2,2560]{1,0:T(2,128)}, u32[]{:S(2)}) copy-start(f32[2,2560]{1,0:T(2,128)} %param.22) | copy-start | bytes 61444
  60.0 50.1 %copy-start.80 = (bf16[2,64]{1,0:T(2,128)(2,1)S(1)}, bf16[2,64]{1,0:T(2,128)(2,1)}, u32[]{:S(2)}) copy-start(bf16[2,64]{1,0:T(2,128)(2,1)} %param.30) | copy-start | bytes 772
  60.0 50.1 %copy-start.81 = (f32[2,64]{1,0:T(2,128)S(1)}, f32[2,64]{1,0:T(2,128)}, u32[]{:S(2)}) copy-start(f32[2,64]{1,0:T(2,128)} %param.33) | copy-start | bytes 1540
  60.0 51.2 %copy-start.76 = (bf16[2,4,64]{2,1,0:T(4,128)(2,1)S(1)}, bf16[2,4,64]{2,1,0:T(4,128)(2,1)}, u32[]{:S(2)}) copy-start(bf16[2,4,64]{2,1,0:T(4,128)(2,1)} %param.29) | copy-start | bytes 3076
  60.0 51.2 %copy-start.47 = (bf16[2,48,3,64]{3,1,2,0:T(8,128)(2,1)S(1)}, bf16[2,48,3,64]{3,1,2,0:T(8,128)(2,1)}, u32[]{:S(2)}) copy-start(bf16[2,48,3,64]{3,1,2,0:T(8,128)(2,1)} %param.36) | copy-start | bytes 110596
  60.0 67.2 %all-gather.5.cloned.1.call-start = ((), (), s32[]{:S(2)}) async-start(), calls=%async_computation.1 | async-start | bytes 2949120 | tf_op jit(solution)/shard_map/all_gather | solution.py:88
  60.8 193.6 %all-reduce.2.cloned.1.call-start = ((), (), s32[]{:S(2)}) async-start(), calls=%async_computation.2 | async-start | bytes 7864320 | tf_op jit(solution)/shard_map/psum | solution.py:158
  77.8 51.5 %copy-start.10 = (bf16[48,3,256]{2,1,0:T(4,128)(2,1)}, bf16[48,3,256]{2,1,0:T(4,128)(2,1)S(1)}, u32[]{:S(2)}) copy-start(bf16[48,3,256]{2,1,0:T(4,128)(2,1)S(1)} %copy.117) | copy-start | bytes 221188
  111.3 149.2 %copy-start.17 = (bf16[48,3,64]{2,0,1:T(8,128)(2,1)}, bf16[48,3,64]{2,0,1:T(8,128)(2,1)S(1)}, u32[]{:S(2)}) copy-start(bf16[48,3,64]{2,0,1:T(8,128)(2,1)S(1)} %get-tuple-element.193) | copy-start | bytes 55300
  119.3 20.1 %copy-start.66 = (f32[48]{0:T(128)}, f32[48]{0:T(128)S(1)}, u32[]{:S(2)}) copy-start(f32[48]{0:T(128)S(1)} %get-tuple-element.238) | copy-start | bytes 580
  119.3 20.1 %copy-start.67 = (f32[48]{0:T(128)}, f32[48]{0:T(128)S(1)}, u32[]{:S(2)}) copy-start(f32[48]{0:T(128)S(1)} %get-tuple-element.239) | copy-start | bytes 580
  119.3 20.1 %copy-start.68 = (f32[48]{0:T(128)}, f32[48]{0:T(128)S(1)}, u32[]{:S(2)}) copy-start(f32[48]{0:T(128)S(1)} %get-tuple-element.240) | copy-start | bytes 580
  119.7 19.8 %copy-start.33 = (f32[48,64]{1,0:T(8,128)}, f32[48,64]{1,0:T(8,128)S(1)}, u32[]{:S(2)}) copy-start(f32[48,64]{1,0:T(8,128)S(1)} %get-tuple-element.183) | copy-start | bytes 36868
  119.7 19.8 %copy-start.34 = (f32[48,64]{1,0:T(8,128)}, f32[48,64]{1,0:T(8,128)S(1)}, u32[]{:S(2)}) copy-start(f32[48,64]{1,0:T(8,128)S(1)} %get-tuple-element.184) | copy-start | bytes 36868
  119.7 19.8 %copy-start.35 = (f32[48,64]{1,0:T(8,128)}, f32[48,64]{1,0:T(8,128)S(1)}, u32[]{:S(2)}) copy-start(f32[48,64]{1,0:T(8,128)S(1)} %get-tuple-element.185) | copy-start | bytes 36868
  164.5 197.4 %reduce-scatter.4.cloned.1.call-start = ((), (), s32[]{:S(2)}) async-start(), calls=%async_computation.4 | async-start | bytes 4423680
  275.9 30.1 %copy-start.74 = (f32[64]{0:T(128)S(1)}, f32[64]{0:T(128)}, u32[]{:S(2)}) copy-start(f32[64]{0:T(128)} %get-tuple-element.209) | copy-start | bytes 772
  (66 other events, 458.7 us)
Sparse Core Ops, SparseCore 0:
  60.1 32.7 all-gather.6
  94.5 32.6 all-gather.4
  164.6 89.6 all-reduce.1
  316.4 45.5 reduce-scatter.3
where the time goes:
time: 374 us; the launch traced here: 372 us
  waiting for transfers between devices  110 us (29%)
  local copies, waits for them, and re-layouts  81.8 us (22%)
  other arithmetic  75.7 us (20%)
  blocking collectives  74.6 us (20%)
  between operations  15.4 us (4%)
  matrix products  14.1 us (4%)
    psum x1, waiting for transfers between devices, local(): total = lax.psum(term, 'heads')  85.9 us
    unnamed x181, local copies, waits for them, and re-layouts  55.4 us
    psum x2, blocking collectives, token_scale(): return rms_scale(lax.psum(local_sq, 'heads'), inner)  30.6 us
    select_n x2, other arithmetic, recur(): kept = jnp.where((accepted == t + 1)[:, None, None], state, kept)  17.3 us
    all_gather x1, blocking collectives, local(): lax.all_gather(conv_bc_state, 'heads', axis=3, tiled=True)  16.7 us
    unnamed x5, waiting for transfers between devices  16.4 us
    all_gather x1, blocking collectives, local(): lax.all_gather(conv_bc_w, 'heads', axis=2, tiled=True)  15.1 us
    unnamed x14, other arithmetic  12.3 us
  transfers between devices with their start and end apart: 4, of which 3 were waited for; matrix products, arithmetic and copies ran while one was open for 13% of the time, Pallas kernels for 0%

commit v1 on v0

--- a/solution.py
+++ b/solution.py
@@ -5,6 +5,12 @@
 
 LAYERS = 2
 EPS = 1e-05
+
+
+def add_all(shard, mesh_axis):
+    terms = lax.all_gather(shard, mesh_axis, axis=0, tiled=False)
+    total = terms.sum(axis=0)
+    return total
 
 
 def rms_scale(total, count):
@@ -50,7 +56,7 @@
 
 
 def token_scale(local_sq, inner):
-    return rms_scale(lax.psum(local_sq, "heads"), inner)
+    return rms_scale(add_all(local_sq, "heads"), inner)
 
 
 def local(

time: 374 us -> 370 us (0.989)
  blocking collectives: 74.6 us -> 69.7 us
    psum x2 -> x0, blocking collectives: 30.6 us -> none  [token_scale(): return rms_scale(lax.psum(local_sq, 'heads'), inner)]
    all_gather x0 -> x2, blocking collectives: none -> 25.8 us  [add_all(): terms = lax.all_gather(shard, mesh_axis, axis=0, tiled=False)]
where the time goes in v1:
time: 370 us; the launch traced here: 368 us
  waiting for transfers between devices  111 us (30%)
  local copies, waits for them, and re-layouts  81.8 us (22%)
  other arithmetic  75.8 us (20%)
  blocking collectives  69.7 us (19%)
  between operations  15.3 us (4%)
  matrix products  14.1 us (4%)
    psum x1, waiting for transfers between devices, local(): total = lax.psum(term, 'heads')  86.1 us
    unnamed x181, local copies, waits for them, and re-layouts  56.3 us
    all_gather x2, blocking collectives, add_all(): terms = lax.all_gather(shard, mesh_axis, axis=0, tiled=False)  25.8 us
    select_n x2, other arithmetic, recur(): kept = jnp.where((accepted == t + 1)[:, None, None], state, kept)  17.2 us
    unnamed x5, waiting for transfers between devices  17 us
    all_gather x1, blocking collectives, local(): lax.all_gather(conv_bc_state, 'heads', axis=3, tiled=True)  16.7 us
    all_gather x1, blocking collectives, local(): lax.all_gather(conv_bc_w, 'heads', axis=2, tiled=True)  15.1 us
    unnamed x14, other arithmetic  12.3 us
  transfers between devices with their start and end apart: 4, of which 3 were waited for; matrix products, arithmetic and copies ran while one was open for 13% of the time, Pallas kernels for 0%

profile of v1, /device:TPU:0, one launch (start us, length us, event | category | flops | bytes accessed | tf_op | source)
XLA Modules:
  0.0 367.9 jit_solution(5121412912445937327)
XLA Ops:
  7.2 43.7 %copy.113 = bf16[50280,320]{1,0:T(8,128)(2,1)} copy(bf16[50280,320]{0,1:T(8,128)(2,1)} %param.21) | data formatting | bytes 64358400 | tf_op args[2]
  51.2 7.8 %gather_fusion = bf16[384,320]{1,0:T(8,128)(2,1)S(1)} fusion(bf16[50280,320]{1,0:T(8,128)(2,1)} %copy.113, s32[1024]{0:T(1024)S(1)} %pad_clamp_fusion), kind=kCustom, calls=%fused_computation | custom fusion | bytes 493056 | tf_op jit(solution)/shard_map/gather | solution.py:153
  60.8 16.7 %all_gather.22 = bf16[2,48,3,256]{1,3,2,0:T(8,128)(2,1)S(1)} all-gather(bf16[2,48,3,32]{1,3,2,0:T(8,128)(2,1)S(1)} %copy-done.48), channel_id=1, replica_groups=mesh['batch'=4,'heads'=8] {'heads'}, dimensions={3}, use_global_device_ids=true | all-gather | bytes 165888 | tf_op jit(solution)/shard_map/all_gather | solution.py:97
  77.9 15.1 %all_gather.24 = bf16[2,4,256]{1,0,2:T(2,128)(2,1)S(1)} all-gather(bf16[2,4,32]{1,0,2:T(2,128)(2,1)S(1)} %copy.118), channel_id=1, replica_groups=mesh['batch'=4,'heads'=8] {'heads'}, dimensions={2}, use_global_device_ids=true | all-gather | bytes 4608 | tf_op jit(solution)/shard_map/all_gather | solution.py:95
  93.0 12.0 %all-gather.1 = bf16[8,32,2]{1,2,0:T(2,128)(2,1)S(1)} all-gather(bf16[1,32,2]{1,2,0:T(2,128)(2,1)S(1)} %bitcast.580), channel_id=1, replica_groups=mesh['batch'=4,'heads'=8] {'heads'}, dimensions={0}, use_global_device_ids=true | all-gather | bytes 1152 | tf_op jit(solution)/shard_map/all_gather | solution.py:96
  107.1 2.9 slice_reduce_fusion.7
  111.3 2.7 copy.115
  119.7 7.5 %all-gather.7.cloned.1.call-done = bf16[2,2560,256]{1,2,0:T(8,128)(2,1)} async-done(((bf16[2,2560,32]{1,2,0:T(8,128)(2,1)}), bf16[2,2560,256]{1,2,0:T(8,128)(2,1)}) %all-gather.7.cloned.1.call-update) | async-done | bytes 2621456 | tf_op jit(solution)/shard_map/all_gather | solution.py:94
  131.2 4.1 %multiply_add_fusion.8 = (f32[1,48,64,128]{3,2,1,0:T(8,128)S(1)}, f32[1,48,64,128]{3,2,1,0:T(8,128)S(1)}, f32[48,64]{1,0:T(8,128)S(1)}, f32[48,64]{1,0:T(8,128)S(1)}) fusion(f32[48,128]{1,0:T(8,128)S(1)} %bitcast.537, f32[48,64]{1,0:T(8,128)S(1)} %get-tuple-element.186, f32[48]{0:T(128)S(1)} %get-tuple-element.237, f32[48,128]{1,0:T(8,128)S(1)} %bitcast.525, ...), kind=kLoop, calls=%fused_computation.43 | loop fusion | flops 7464960 | bytes 4977600 | tf_op jit(solution)/shard_map/vmap()/add | solution.py:43
  139.5 3.7 %multiply_reduce_fusion.8 = (f32[48,64]{1,0:T(8,128)S(1)}, f32[48,64]{1,0:T(8,128)S(1)}, f32[48,64]{1,0:T(8,128)S(1)}, f32[48,64]{1,0:T(8,128)S(1)}) fusion(f32[1,48,64,128]{3,2,1,0:T(8,128)S(1)} %get-tuple-element.86, f32[48,128]{1,0:T(8,128)S(1)} %bitcast.566, f32[48,128]{1,0:T(8,128)S(1)} %bitcast.535, f32[48,64]{1,0:T(8,128)S(1)} %get-tuple-element.184, ...), kind=kLoop, calls=%fused_computation.37 | loop fusion | flops 6672384 | bytes 1831488 | tf_op jit(solution)/shard_map/vmap()/reduce_sum | solution.py:46
  145.9 12.8 %all-gather.2 = f32[8,1,384]{2,1,0:T(1,128)S(1)} all-gather(f32[1,1,384]{2,1,0:T(1,128)S(1)} %reshape.2536), channel_id=1, replica_groups=mesh['batch'=4,'heads'=8] {'heads'}, dimensions={0}, use_global_device_ids=true | all-gather | bytes 13824 | tf_op jit(solution)/shard_map/all_gather | solution.py:11
  158.8 3.5 convolution_multiply_fusion.1
  163.4 2.9 slice_reduce_fusion.3
  166.3 86.1 %all-reduce.2.cloned.1.call-done = f32[384,2560]{1,0:T(8,128)} async-done(((f32[384,2560]{1,0:T(8,128)}), f32[384,2560]{1,0:T(8,128)}) %all-reduce.2.cloned.1.call-update) | async-done | bytes 3932176 | tf_op jit(solution)/shard_map/psum | solution.py:164
  252.4 2.9 fusion.1
  262.7 2.1 fusion.14
  266.9 4.1 %multiply_add_fusion.2 = (f32[1,48,64,128]{3,2,1,0:T(8,128)S(1)}, f32[1,48,64,128]{3,2,1,0:T(8,128)S(1)}, f32[48,64]{1,0:T(8,128)S(1)}, f32[48,64]{1,0:T(8,128)S(1)}) fusion(f32[48,128]{1,0:T(8,128)S(1)} %bitcast.551, f32[48,64]{1,0:T(8,128)S(1)} %get-tuple-element.160, f32[48]{0:T(128)S(1)} %get-tuple-element.51, f32[48,128]{1,0:T(8,128)S(1)} %bitcast.528, ...), kind=kLoop, calls=%fused_computation.29 | loop fusion | flops 7464960 | bytes 4977600 | tf_op jit(solution)/shard_map/vmap()/add | solution.py:43
  277.6 3.7 %multiply_reduce_fusion = (f32[48,64]{1,0:T(8,128)S(1)}, f32[48,64]{1,0:T(8,128)S(1)}, f32[48,64]{1,0:T(8,128)S(1)}, f32[48,64]{1,0:T(8,128)S(1)}) fusion(f32[1,48,64,128]{3,2,1,0:T(8,128)S(1)} %get-tuple-element.82, f32[48,128]{1,0:T(8,128)S(1)} %bitcast.562, f32[48,128]{1,0:T(8,128)S(1)} %bitcast.549, f32[48,64]{1,0:T(8,128)S(1)} %bitcast_multiply_fusion.2, ...), kind=kLoop, calls=%fused_computation.23 | loop fusion | flops 6672384 | bytes 1831488 | tf_op jit(solution)/shard_map/vmap()/reduce_sum | solution.py:46
  288.4 13.1 %all-gather.3 = f32[8,1,384]{2,1,0:T(1,128)S(1)} all-gather(f32[1,1,384]{2,1,0:T(1,128)S(1)} %reshape.2538), channel_id=1, replica_groups=mesh['batch'=4,'heads'=8] {'heads'}, dimensions={0}, use_global_device_ids=true | all-gather | bytes 13824 | tf_op jit(solution)/shard_map/all_gather | solution.py:11
  302.6 3.5 fusion
  306.1 5.6 %copy.139 = f32[2560,384]{1,0:T(8,128)} copy(f32[2560,384]{0,1:T(8,128)} %fusion) | data formatting | bytes 7864320
  317.5 9.0 %select_select_fusion.1 = f32[1,48,1,64,128]{4,3,2,1,0:T(8,128)} fusion(f32[2,48,1,64,128]{4,3,2,1,0:T(8,128)S(1)} %copy-done.1, f32[48,128]{1,0:T(8,128)} %bitcast.536, f32[48,64]{1,0:T(8,128)} %copy-done.34, f32[48,128]{1,0:T(8,128)} %bitcast.534, f32[48,64]{1,0:T(8,128)} %copy-done.35, f32[48,128]{1,0:T(8,128)} %bitcast.532, f32[48,64]{1,0:T(8,128)} %copy-done.33, ...), kind=kLoop, calls=%fused_computation.22 | loop fusion | flops 12582912 | bytes 3442560 | tf_op jit(solution)/shard_map/vmap(jit(_where))/select_n | solution.py:47
  331.6 8.2 %select_select_fusion = f32[1,48,1,64,128]{4,3,2,1,0:T(8,128)S(1)} fusion(f32[2,48,1,64,128]{4,3,2,1,0:T(8,128)S(1)} %copy-done.1, f32[48,128]{1,0:T(8,128)} %bitcast.550, f32[48,64]{1,0:T(8,128)} %copy-done.40, f32[48,128]{1,0:T(8,128)} %bitcast.548, f32[48,64]{1,0:T(8,128)} %copy-done.42, f32[48,128]{1,0:T(8,128)} %bitcast.546, f32[48,64]{1,0:T(8,128)} %copy-done.41, ...), kind=kLoop, calls=%fused_computation.21 | loop fusion | flops 12582912 | bytes 3442560 | tf_op jit(solution)/shard_map/vmap(jit(_where))/select_n | solution.py:47
  341.8 16.3 %reduce-scatter.4.cloned.1.call-done = f32[320,384]{1,0:T(8,128)} async-done(((f32[2560,384]{1,0:T(8,128)}), f32[320,384]{1,0:T(8,128)}) %reduce-scatter.4.cloned.1.call-update) | async-done | bytes 491536
  (283 shorter events, 62.2 us)
Async XLA Ops:
  7.2 43.8 %copy-start.73 = (s32[48,8]{0,1:T(8,128)S(1)}, s32[48,8]{0,1:T(8,128)}, u32[]{:S(2)}) copy-start(s32[48,8]{0,1:T(8,128)} %param.19) | copy-start | bytes 4612
  7.2 104.1 %all-gather.9.cloned.1.call-start = ((), (), s32[]{:S(2)}) async-start(), calls=%async_computation.3 | async-start | bytes 2211840 | tf_op jit(solution)/shard_map/all_gather | solution.py:154
  59.0 18.7 %copy-start.74 = (bf16[2,4,32]{2,1,0:T(4,128)(2,1)S(1)}, bf16[2,4,32]{2,1,0:T(4,128)(2,1)}, u32[]{:S(2)}) copy-start(bf16[2,4,32]{2,1,0:T(4,128)(2,1)} %param.31) | copy-start | bytes 1540
  59.0 34.0 %copy-start.81 = (bf16[2,32]{1,0:T(2,128)(2,1)S(1)}, bf16[2,32]{1,0:T(2,128)(2,1)}, u32[]{:S(2)}) copy-start(bf16[2,32]{1,0:T(2,128)(2,1)} %param.32) | copy-start | bytes 388
  59.0 46.1 %copy-start.76 = (f32[2,1]{0,1:T(1,128)S(1)}, f32[2,1]{0,1:T(1,128)}, u32[]{:S(2)}) copy-start(f32[2,1]{0,1:T(1,128)} %param.26) | copy-start | bytes 28
  59.0 46.7 %copy-start.77 = (f32[2,1]{0,1:T(1,128)S(1)}, f32[2,1]{0,1:T(1,128)}, u32[]{:S(2)}) copy-start(f32[2,1]{0,1:T(1,128)} %param.27) | copy-start | bytes 28
  59.1 47.3 %copy-start.78 = (f32[2,1]{0,1:T(1,128)S(1)}, f32[2,1]{0,1:T(1,128)}, u32[]{:S(2)}) copy-start(f32[2,1]{0,1:T(1,128)} %param.28) | copy-start | bytes 28
  59.1 47.8 %copy-start.55 = (f32[2,2560]{1,0:T(2,128)S(1)}, f32[2,2560]{1,0:T(2,128)}, u32[]{:S(2)}) copy-start(f32[2,2560]{1,0:T(2,128)} %param.22) | copy-start | bytes 61444
  60.0 50.1 %copy-start.79 = (bf16[2,64]{1,0:T(2,128)(2,1)S(1)}, bf16[2,64]{1,0:T(2,128)(2,1)}, u32[]{:S(2)}) copy-start(bf16[2,64]{1,0:T(2,128)(2,1)} %param.30) | copy-start | bytes 772
  60.0 50.1 %copy-start.80 = (f32[2,64]{1,0:T(2,128)S(1)}, f32[2,64]{1,0:T(2,128)}, u32[]{:S(2)}) copy-start(f32[2,64]{1,0:T(2,128)} %param.33) | copy-start | bytes 1540
  60.0 51.2 %copy-start.75 = (bf16[2,4,64]{2,1,0:T(4,128)(2,1)S(1)}, bf16[2,4,64]{2,1,0:T(4,128)(2,1)}, u32[]{:S(2)}) copy-start(bf16[2,4,64]{2,1,0:T(4,128)(2,1)} %param.29) | copy-start | bytes 3076
  60.0 51.2 %copy-start.47 = (bf16[2,48,3,64]{3,1,2,0:T(8,128)(2,1)S(1)}, bf16[2,48,3,64]{3,1,2,0:T(8,128)(2,1)}, u32[]{:S(2)}) copy-start(bf16[2,48,3,64]{3,1,2,0:T(8,128)(2,1)} %param.36) | copy-start | bytes 110596
  60.0 67.2 %all-gather.7.cloned.1.call-start = ((), (), s32[]{:S(2)}) async-start(), calls=%async_computation.1 | async-start | bytes 2949120 | tf_op jit(solution)/shard_map/all_gather | solution.py:94
  60.8 191.6 %all-reduce.2.cloned.1.call-start = ((), (), s32[]{:S(2)}) async-start(), calls=%async_computation.2 | async-start | bytes 7864320 | tf_op jit(solution)/shard_map/psum | solution.py:164
  77.8 51.5 %copy-start.10 = (bf16[48,3,256]{2,1,0:T(4,128)(2,1)}, bf16[48,3,256]{2,1,0:T(4,128)(2,1)S(1)}, u32[]{:S(2)}) copy-start(bf16[48,3,256]{2,1,0:T(4,128)(2,1)S(1)} %copy.117) | copy-start | bytes 221188
  111.3 147.2 %copy-start.17 = (bf16[48,3,64]{2,0,1:T(8,128)(2,1)}, bf16[48,3,64]{2,0,1:T(8,128)(2,1)S(1)}, u32[]{:S(2)}) copy-start(bf16[48,3,64]{2,0,1:T(8,128)(2,1)S(1)} %get-tuple-element.193) | copy-start | bytes 55300
  119.3 16.7 %copy-start.56 = (f32[48]{0:T(128)}, f32[48]{0:T(128)S(1)}, u32[]{:S(2)}) copy-start(f32[48]{0:T(128)S(1)} %get-tuple-element.236) | copy-start | bytes 580
  119.3 20.1 %copy-start.66 = (f32[48]{0:T(128)}, f32[48]{0:T(128)S(1)}, u32[]{:S(2)}) copy-start(f32[48]{0:T(128)S(1)} %get-tuple-element.238) | copy-start | bytes 580
  119.3 20.1 %copy-start.67 = (f32[48]{0:T(128)}, f32[48]{0:T(128)S(1)}, u32[]{:S(2)}) copy-start(f32[48]{0:T(128)S(1)} %get-tuple-element.239) | copy-start | bytes 580
  119.3 20.1 %copy-start.68 = (f32[48]{0:T(128)}, f32[48]{0:T(128)S(1)}, u32[]{:S(2)}) copy-start(f32[48]{0:T(128)S(1)} %get-tuple-element.240) | copy-start | bytes 580
  119.7 19.8 %copy-start.33 = (f32[48,64]{1,0:T(8,128)}, f32[48,64]{1,0:T(8,128)S(1)}, u32[]{:S(2)}) copy-start(f32[48,64]{1,0:T(8,128)S(1)} %get-tuple-element.183) | copy-start | bytes 36868
  119.7 19.8 %copy-start.34 = (f32[48,64]{1,0:T(8,128)}, f32[48,64]{1,0:T(8,128)S(1)}, u32[]{:S(2)}) copy-start(f32[48,64]{1,0:T(8,128)S(1)} %get-tuple-element.184) | copy-start | bytes 36868
  119.7 19.8 %copy-start.35 = (f32[48,64]{1,0:T(8,128)}, f32[48,64]{1,0:T(8,128)S(1)}, u32[]{:S(2)}) copy-start(f32[48,64]{1,0:T(8,128)S(1)} %get-tuple-element.185) | copy-start | bytes 36868
  162.3 195.7 %reduce-scatter.4.cloned.1.call-start = ((), (), s32[]{:S(2)}) async-start(), calls=%async_computation.4 | async-start | bytes 4423680
  (65 other events, 441.8 us)
Sparse Core Ops, SparseCore 0:
  60.1 32.7 all-gather.8
  94.5 32.6 all-gather.6
  162.4 89.9 all-reduce.1
  311.8 46.1 reduce-scatter.3
